TPU v7x, 32 devices: a whole 2x2x4 slice. The times are simulated.
32 devices in a mesh: lat: 16 (over z, y, core), lon: 2 (over x).
Axes of the slice: x: 2, y: 2, z: 4, core: 2. Of those that a mesh axis runs over, the one named last changes fastest.
Arguments:
- eastward_speed_face: float32 [72, 512, 256], P(None, 'lat', 'lon'), may hold values from -6 to 6
- northward_speed_face: float32 [72, 512, 256], P(None, 'lat', 'lon'), may hold values from -6 to 6
- stratum_extent_east_face: float32 [72, 512, 256], P(None, 'lat', 'lon'), may hold values from 0.5 to 2
- stratum_extent_north_face: float32 [72, 512, 256], P(None, 'lat', 'lon'), may hold values from 0.5 to 2
- northward_span_east_face: float32 [512, 256], P('lat', 'lon'), may hold values from 0.5 to 2
- eastward_span_north_face: float32 [512, 256], P('lat', 'lon'), may hold values from 0.5 to 2
- ocean_flag_east_face: int32 [72, 512, 256], P(None, 'lat', 'lon'), may hold values 0 or 1
- ocean_flag_north_face: int32 [72, 512, 256], P(None, 'lat', 'lon'), may hold values 0 or 1
- counterpart_across_seam: int32 [256], replicated, may hold values from 0 to 255, as said below
Outputs:
- eastward_speed_next: float32 [72, 512, 256], P(None, 'lat', 'lon')
- northward_speed_next: float32 [72, 512, 256], P(None, 'lat', 'lon')
Inputs may be any that keep to these rules, and one draw needn't show every extreme that they name: counterpart_across_seam[i] = (p - 1 - i) mod 256 for one pivot p drawn anew in each draw; it is its own inverse.
All inputs are finite; a program needn't handle non-finite values. No bound on the sum of `ocean_flag_east_face` or of `ocean_flag_north_face` on one device may be relied on, other than what follows from the above.
Results may differ from a plain program's by a relative error of at most 0.00002.
Values sent between devices are 32-bit elements; how exact they have to be, the bound alone decides.
A program may use at most 128 MiB of HBM per device.

v0:
```python
import jax
import jax.numpy as jnp
from jax import lax
from jax.sharding import PartitionSpec as P

time_step = 0.2


def extended_2(block, sides, width, periodic):
    for axis, dim in sides:
        count = lax.axis_size(axis)
        forward = [(i, i + 1) for i in range(count - 1)]
        if periodic:
            forward.append((count - 1, 0))
        backward = [(target, source) for source, target in forward]
        low = lax.ppermute(
            lax.slice_in_dim(block, block.shape[dim] - width, None, axis=dim), axis, forward
        )
        high = lax.ppermute(lax.slice_in_dim(block, 0, width, axis=dim), axis, backward)
        block = jnp.concatenate([low, block, high], axis=dim)
    return block


def interp(a, b, c, d):
    return (7.0 * (b + c) - (a + d)) / 12.0


def advect(umv, vmv, tuv, tvv, rows, cols):

    def cx(field, ro, co):
        return field[..., ro : ro + rows, co : co + cols + 1]

    def ry(field, ro, co):
        return field[..., ro : ro + rows + 1, co : co + cols]

    fut = (
        0.5
        * (cx(tuv, 2, 1) + cx(tuv, 2, 2))
        * interp(cx(umv, 2, 0), cx(umv, 2, 1), cx(umv, 2, 2), cx(umv, 2, 3))
    )
    vface = ry(tvv, 1, 2)
    fvf = (
        0.5
        * (vface + ry(tvv, 1, 3))
        * interp(ry(umv, 0, 2), ry(umv, 1, 2), ry(umv, 2, 2), ry(umv, 3, 2))
    )
    fuf = (
        0.5
        * (cx(tuv, 2, 1) + cx(tuv, 3, 1))
        * interp(cx(vmv, 2, 0), cx(vmv, 2, 1), cx(vmv, 2, 2), cx(vmv, 2, 3))
    )
    fvt = (
        0.5
        * (vface + ry(tvv, 2, 2))
        * interp(ry(vmv, 0, 2), ry(vmv, 1, 2), ry(vmv, 2, 2), ry(vmv, 3, 2))
    )
    trend_u = -(fut[..., 1:] - fut[..., :-1] + (fvf[..., 1:, :] - fvf[..., :-1, :]))
    trend_v = -(fuf[..., 1:] - fuf[..., :-1] + (fvt[..., 1:, :] - fvt[..., :-1, :]))
    return (trend_u, trend_v)


def place_fold(extended, ghosts):
    at_top = lax.axis_index("lat") == lax.axis_size("lat") - 1
    height = extended.shape[2]
    upper = extended[:, :, height - 2 :, :]
    top_rows = jnp.where(at_top, ghosts, upper)
    return lax.dynamic_update_slice_in_dim(extended, top_rows, height - 2, 2)


def local(
    eastward_speed_face,
    northward_speed_face,
    stratum_extent_east_face,
    stratum_extent_north_face,
    northward_span_east_face,
    eastward_span_north_face,
    ocean_flag_east_face,
    ocean_flag_north_face,
    counterpart_across_seam,
):
    umf = ocean_flag_east_face.astype(jnp.float32)
    northward_transport_rate = ocean_flag_north_face.astype(jnp.float32)
    um = umf * eastward_speed_face
    vm = northward_transport_rate * northward_speed_face
    volu = northward_span_east_face[None] * stratum_extent_east_face
    volv = eastward_span_north_face[None] * stratum_extent_north_face
    fields = jnp.stack([um, vm, volu * um, volv * vm])
    rows = um.shape[1]
    cols = um.shape[2]
    tall = extended_2(fields, (("lat", 2),), 2, False)
    band = lax.all_gather(fields[:, :, -2:, :], "lon", axis=3, tiled=True)
    own_columns = lax.axis_index("lon") * cols + jnp.arange(cols, dtype=jnp.int32)
    ghosts = -jnp.take(band[:, :, ::-1, :], counterpart_across_seam[own_columns], axis=3)
    tall = place_fold(tall, ghosts)
    extended = extended_2(tall, (("lon", 3),), 2, True)
    trend_u, trend_v = advect(extended[0], extended[1], extended[2], extended[3], rows, cols)
    eastward_speed_next = umf * (um + time_step * trend_u / volu)
    northward_speed_next = northward_transport_rate * (vm + time_step * trend_v / volv)
    return (eastward_speed_next, northward_speed_next)


def solution(mesh):
    return jax.shard_map(
        local,
        mesh=mesh,
        in_specs=(
            P(None, "lat", "lon"),
            P(None, "lat", "lon"),
            P(None, "lat", "lon"),
            P(None, "lat", "lon"),
            P("lat", "lon"),
            P("lat", "lon"),
            P(None, "lat", "lon"),
            P(None, "lat", "lon"),
            P(),
        ),
        out_specs=(P(None, "lat", "lon"), P(None, "lat", "lon")),
        check_vma=False,
    )
```

profile of v0, /device:TPU:0, one launch (start us, length us, event | category | flops | bytes accessed | tf_op | source)
XLA Modules:
  0.0 111.4 jit_solution(351955340508635767)
XLA Ops:
  0.6 0.0 copy-start
  0.6 0.0 copy-start.11
  0.7 0.9 copy.165
  1.6 0.8 copy.167
  2.4 3.1 %copy.166 = f32[72,32,128]{0,1,2:T(8,128)} copy(f32[72,32,128]{2,1,0:T(8,128)} %param.11) | data formatting | bytes 2359296 | tf_op args[2]
  5.5 0.0 copy-done.11
  5.5 0.0 copy-start.12
  5.5 2.1 %copy.168 = f32[72,32,128]{0,1,2:T(8,128)} copy(f32[72,32,128]{2,1,0:T(8,128)S(1)} %copy-done.11) | data formatting | bytes 2359296 | tf_op args[3]
  7.6 0.0 copy-done.12
  7.6 0.0 copy-start.13
  7.6 2.2 %copy.161 = s32[72,32,128]{0,1,2:T(8,128)} copy(s32[72,32,128]{2,1,0:T(8,128)S(1)} %copy-done.12) | data formatting | bytes 2359296 | tf_op args[6]
  9.7 0.0 copy-done.13
  9.7 2.1 %copy.163 = s32[72,32,128]{0,1,2:T(8,128)} copy(s32[72,32,128]{2,1,0:T(8,128)S(1)} %copy-done.13) | data formatting | bytes 2359296 | tf_op args[7]
  11.9 0.0 copy-done.14
  11.9 0.0 copy-start.15
  11.9 2.1 %copy.162 = f32[72,32,128]{0,1,2:T(8,128)} copy(f32[72,32,128]{2,1,0:T(8,128)S(1)} %copy-done.14) | data formatting | bytes 2359296 | tf_op args[0]
  14.0 0.0 copy-done.15
  14.0 2.1 %copy.164 = f32[72,32,128]{0,1,2:T(8,128)} copy(f32[72,32,128]{2,1,0:T(8,128)S(1)} %copy-done.15) | data formatting | bytes 2359296 | tf_op args[1]
  16.0 0.0 copy-start.6
  16.0 0.0 copy-start.8
  16.0 0.0 copy-start.10
  16.0 3.4 %multiply_multiply_fusion = (f32[72,32,128]{0,1,2:T(8,128)S(1)}, f32[72,32,128]{0,1,2:T(8,128)S(1)}) fusion(f32[72,32,128]{0,1,2:T(8,128)} %copy.168, f32[32,128]{0,1:T(8,128)S(1)} %copy.167, f32[72,32,128]{0,1,2:T(8,128)} %copy.164, s32[72,32,128]{0,1,2:T(8,128)} %copy.163), kind=kLoop, calls=%fused_computation.58 | loop fusion | flops 1179648 | bytes 5914624 | tf_op jit(solution)/shard_map/mul | solution.py:87
  19.4 0.1 copy-done.6
  19.5 0.6 copy-done.8
  20.1 0.6 copy-done.10
  20.8 0.0 copy-start.4
  20.8 0.8 multiply_multiply_fusion.1
  21.6 0.0 copy-start.2
  21.6 0.0 copy-start.5
  21.6 0.5 copy-done.4
  22.1 2.2 %pad_maximum_fusion.5 = (f32[4,72,2,128]{1,0,2,3:T(4,128)}, f32[4,72,2,128]{1,0,2,3:T(4,128)}) fusion(f32[1,72,32,128]{1,0,2,3:T(1,128)S(1)} %bitcast.36, f32[1,72,32,128]{1,0,2,3:T(1,128)S(1)} %bitcast.38, f32[1,72,32,128]{1,0,2,3:T(1,128)S(1)} %bitcast.32, f32[1,72,32,128]{1,0,2,3:T(1,128)S(1)} %bitcast.34), kind=kLoop, calls=%fused_computation.63 | loop fusion | flops 442368 | bytes 5308416 | tf_op jit(solution)/shard_map/slice | solution.py:17
  24.3 0.0 copy-done.2
  24.3 0.0 copy-done.5
  24.3 1.3 %collective-permute-start.1 = (f32[4,72,2,128]{1,0,2,3:T(4,128)}, f32[4,72,2,128]{1,0,2,3:T(4,128)}, u32[]{:S(2)}, u32[]{:S(2)}) collective-permute-start(f32[4,72,2,128]{1,0,2,3:T(4,128)} %get-tuple-element.25), channel_id=1, source_target_pairs={{2,0},{4,2},{6,4},{8,6},{10,8},{12,10},{14,12},{16,14},{18,16},{20... | collective-permute-start | bytes 884744 | tf_op jit(solution)/shard_map/ppermute | solution.py:19
  25.6 3.8 %collective-permute-start = (f32[4,72,2,128]{1,0,2,3:T(4,128)}, f32[4,72,2,128]{1,0,2,3:T(4,128)}, u32[]{:S(2)}, u32[]{:S(2)}) collective-permute-start(f32[4,72,2,128]{1,0,2,3:T(4,128)} %get-tuple-element.24), channel_id=1, source_target_pairs={{0,2},{2,4},{4,6},{6,8},{8,10},{10,12},{12,14},{14,16},{16,18},{18... | collective-permute-start | bytes 884744 | tf_op jit(solution)/shard_map/ppermute | solution.py:16
  29.4 1.2 %copy.172 = f32[4,72,2,128]{3,1,2,0:T(8,128)S(1)} copy(f32[4,72,2,128]{1,0,2,3:T(4,128)} %get-tuple-element.24) | data formatting | bytes 589824 | tf_op jit(solution)/shard_map/slice | solution.py:17
  30.7 0.0 copy-done
  30.7 1.3 %gather_fusion = s32[128]{0:T(128)S(1)} fusion(s32[256]{0:T(256)S(1)} %copy-done, s32[1024]{0:T(1024)S(1)} %pad_clamp_fusion.1), kind=kCustom, calls=%fused_computation | custom fusion | bytes 1536 | tf_op jit(solution)/shard_map/gather | solution.py:93
  32.0 11.5 %all_gather.3 = f32[4,72,2,256]{3,1,2,0:T(8,128)} all-gather(f32[4,72,2,128]{3,1,2,0:T(8,128)S(1)} %copy.172), channel_id=1, replica_groups=mesh['lat'=16,'lon'=2] {'lon'}, dimensions={3}, use_global_device_ids=true | all-gather | bytes 884736 | tf_op jit(solution)/shard_map/all_gather | solution.py:91
  43.5 1.4 %copy.173 = f32[4,72,2,256]{1,0,3,2:T(4,128)S(1)} copy(f32[4,72,2,256]{3,1,2,0:T(8,128)} %all_gather.3) | data formatting | bytes 1179648 | tf_op jit(solution)/shard_map/all_gather | solution.py:91
  45.0 1.0 rev.3
  46.0 2.2 %gather_fusion.1 = f32[128,4,72,2]{2,1,3,0:T(4,128)S(1)} fusion(f32[4,72,2,256]{1,0,3,2:T(4,128)} %rev.3, s32[1024]{0:T(1024)S(1)} %pad_clamp_fusion), kind=kCustom, calls=%fused_computation.1 | custom fusion | bytes 590336 | tf_op jit(solution)/shard_map/jit(_take)/gather | solution.py:93
  48.2 0.0 collective-permute-done.1
  48.2 0.0 collective-permute-done
  48.2 11.8 %pad_maximum_fusion.1 = f32[4,72,36,128]{1,0,2,3:T(4,128)S(1)} fusion(f32[4,72,2,128]{1,0,2,3:T(4,128)} %collective-permute-done.1, f32[1,72,32,128]{1,0,2,3:T(1,128)} %bitcast.37, f32[1,72,32,128]{1,0,2,3:T(1,128)} %bitcast.39, f32[1,72,32,128]{1,0,2,3:T(1,128)S(1)} %bitcast.33, f32[1,72,32,128]{1,0,2,3:T(1,128)} %bitcast.35, ...), kind=kLoop, calls=%fused_computation.3 | loop fusion | flops 6635520 | bytes 10616832 | tf_op jit(solution)/shard_map/concatenate | solution.py:20
  60.0 1.4 %fusion.32 = f32[4,72,36,128]{1,0,2,3:T(4,128)S(1)} fusion(f32[4,72,36,128]{1,0,2,3:T(4,128)S(1)} %pad_maximum_fusion.1, f32[4,72,2,128]{1,0,2,3:T(4,128)} %collective-permute-done.1, f32[128,4,72,2]{2,1,3,0:T(4,128)S(1)} %gather_fusion.1, pred[128]{0:T(512)(128)(4,1)S(1)} %compare_and_fusion, pred[]{:T(512)S(6)} %eq.3), kind=kLoop, calls=%fused_computation.65 | loop fusion | flops 221184 | bytes 1344001 | tf_op jit(solution)/shard_map/dynamic_update_slice | solution.py:67
  61.4 1.6 %collective-permute-start.2 = (f32[4,72,36,2]{1,0,2,3:T(4,128)S(1)}, f32[4,72,36,2]{1,0,2,3:T(4,128)S(1)}, u32[]{:S(2)}, u32[]{:S(2)}) collective-permute-start(f32[4,72,36,2]{1,0,2,3:T(4,128)S(1)} %get-tuple-element.22), channel_id=1, source_target_pairs={{0,1},{1,0},{2,3},{3,2},{4,5},{5,4},{6,7},{7,6},{8,9},{9,8},{10,11... | collective-permute-start | bytes 248840 | tf_op jit(solution)/shard_map/ppermute | solution.py:16
  63.0 0.5 collective-permute-start.3
  63.5 4.7 %collective-permute-done.2 = f32[4,72,36,2]{1,0,2,3:T(4,128)S(1)} collective-permute-done((f32[4,72,36,2]{1,0,2,3:T(4,128)S(1)}, f32[4,72,36,2]{1,0,2,3:T(4,128)S(1)}, u32[]{:S(2)}, u32[]{:S(2)}) %collective-permute-start.2) | collective-permute-done | bytes 82976 | tf_op jit(solution)/shard_map/ppermute | solution.py:16
  68.2 2.2 %collective-permute-done.3 = f32[4,72,36,2]{1,0,2,3:T(4,128)S(1)} collective-permute-done((f32[4,72,36,2]{1,0,2,3:T(4,128)S(1)}, f32[4,72,36,2]{1,0,2,3:T(4,128)S(1)}, u32[]{:S(2)}, u32[]{:S(2)}) %collective-permute-start.3) | collective-permute-done | bytes 82976 | tf_op jit(solution)/shard_map/ppermute | solution.py:19
  70.4 8.5 %pad_maximum_fusion = f32[4,72,36,132]{1,0,2,3:T(4,128)S(1)} fusion(f32[4,72,36,2]{1,0,2,3:T(4,128)S(1)} %collective-permute-done.3, f32[4,72,36,128]{1,0,2,3:T(4,128)S(1)} %fusion.32, f32[4,72,36,2]{1,0,2,3:T(4,128)S(1)} %collective-permute-done.2), kind=kLoop, calls=%fused_computation.2 | loop fusion | flops 2737152 | bytes 10948608 | tf_op jit(solution)/shard_map/concatenate | solution.py:20
  78.9 7.2 %fusion.35 = (f32[1,72,36,132]{1,0,2,3:T(1,128)S(1)}, f32[1,72,36,132]{1,0,2,3:T(1,128)S(1)}, f32[1,72,36,132]{1,0,2,3:T(1,128)S(1)}, f32[1,72,36,132]{1,0,2,3:T(1,128)S(1)}) fusion(f32[4,72,36,132]{1,0,2,3:T(4,128)S(1)} %pad_maximum_fusion), kind=kLoop, calls=%fused_computation.74 | loop fusion | bytes 10948608 | tf_op jit(solution)/shard_map/slice | solution.py:96
  86.1 0.4 copy_bitcast_fusion
  86.4 0.4 copy_bitcast_fusion.2
  86.8 4.7 %fusion.12 = (f32[72,32,129]{0,1,2:T(8,128)}, f32[72,32,129]{0,1,2:T(8,128)S(1)}) fusion(f32[72,36,132]{0,1,2:T(8,128)S(1)} %get-tuple-element.30, f32[72,36,132]{0,1,2:T(8,128)S(1)} %get-tuple-element.33, f32[72,36,132]{0,1,2:T(8,128)S(1)} %get-tuple-element.32), kind=kLoop, calls=%fused_computation.27 | loop fusion | flops 4755456 | bytes 15455232 | tf_op jit(solution)/shard_map/mul | solution.py:48
  91.5 4.1 %fusion.2 = (f32[72,33,128]{0,1,2:T(8,128)}, f32[72,33,128]{0,1,2:T(8,128)S(1)}) fusion(f32[72,36,132]{0,1,2:T(8,128)S(1)} %get-tuple-element.30, f32[72,36,132]{0,1,2:T(8,128)S(1)} %get-tuple-element.31, f32[72,36,132]{0,1,2:T(8,128)S(1)} %get-tuple-element.32), kind=kLoop, calls=%fused_computation.11 | loop fusion | flops 4866048 | bytes 15814656 | tf_op jit(solution)/shard_map/mul | solution.py:53
  95.6 0.0 copy-done.3
  95.6 0.0 copy-done.7
  95.6 0.0 copy-done.9
  95.6 2.6 %fusion.31 = f32[72,32,128]{0,1,2:T(8,128)} fusion(f32[72,32,128]{0,1,2:T(8,128)S(1)} %copy-done.3, f32[72,33,128]{0,1,2:T(8,128)S(1)} %get-tuple-element.29, f32[72,32,129]{0,1,2:T(8,128)S(1)} %get-tuple-element.27, s32[72,32,128]{0,1,2:T(8,128)S(1)} %copy-done.9, f32[72,32,128]{0,1,2:T(8,128)S(1)} %copy-done.7, f32[32,128]{0,1:T(8,128)S(1)} %copy.165), kind=kLoop, calls=%fused_computation.54 | loop fusion | flops 2949120 | bytes 9453568 | tf_op jit(solution)/shard_map/mul | solution.py:97
  98.2 3.1 %copy.200 = f32[72,32,128]{2,1,0:T(8,128)} copy(f32[72,32,128]{0,1,2:T(8,128)} %fusion.31) | data formatting | bytes 2359296
  101.3 7.0 %fusion.25 = f32[72,32,128]{0,1,2:T(8,128)} fusion(f32[72,32,128]{0,1,2:T(8,128)S(1)} %get-tuple-element.17, f32[72,33,128]{0,1,2:T(8,128)} %get-tuple-element.28, f32[72,32,129]{0,1,2:T(8,128)} %get-tuple-element.26, s32[72,32,128]{0,1,2:T(8,128)} %copy.163, f32[72,32,128]{0,1,2:T(8,128)} %copy.168, f32[32,128]{0,1:T(8,128)S(1)} %copy.167), kind=kLoop, calls=%fused_computation.46 | loop fusion | flops 2949120 | bytes 9453568 | tf_op jit(solution)/shard_map/mul | solution.py:98
  108.3 3.1 %copy.201 = f32[72,32,128]{2,1,0:T(8,128)} copy(f32[72,32,128]{0,1,2:T(8,128)} %fusion.25) | data formatting | bytes 2359296
  111.4 0.0 copy-done.1
  (11 shorter events, 0.1 us)
Async XLA Ops:
  0.6 30.1 %copy-start = (s32[256]{0:T(256)S(1)}, s32[256]{0:T(256)}, u32[]{:S(2)}) copy-start(s32[256]{0:T(256)} %param.17) | copy-start | bytes 3076
  0.6 4.9 %copy-start.11 = (f32[72,32,128]{2,1,0:T(8,128)S(1)}, f32[72,32,128]{2,1,0:T(8,128)}, u32[]{:S(2)}) copy-start(f32[72,32,128]{2,1,0:T(8,128)} %param.12) | copy-start | bytes 3538948
  5.5 2.1 %copy-start.12 = (s32[72,32,128]{2,1,0:T(8,128)S(1)}, s32[72,32,128]{2,1,0:T(8,128)}, u32[]{:S(2)}) copy-start(s32[72,32,128]{2,1,0:T(8,128)} %param.15) | copy-start | bytes 3538948
  7.6 2.2 %copy-start.13 = (s32[72,32,128]{2,1,0:T(8,128)S(1)}, s32[72,32,128]{2,1,0:T(8,128)}, u32[]{:S(2)}) copy-start(s32[72,32,128]{2,1,0:T(8,128)} %param.16) | copy-start | bytes 3538948
  9.7 2.1 %copy-start.14 = (f32[72,32,128]{2,1,0:T(8,128)S(1)}, f32[72,32,128]{2,1,0:T(8,128)}, u32[]{:S(2)}) copy-start(f32[72,32,128]{2,1,0:T(8,128)} %param.9) | copy-start | bytes 3538948
  11.9 2.1 %copy-start.15 = (f32[72,32,128]{2,1,0:T(8,128)S(1)}, f32[72,32,128]{2,1,0:T(8,128)}, u32[]{:S(2)}) copy-start(f32[72,32,128]{2,1,0:T(8,128)} %param.10) | copy-start | bytes 3538948
  16.0 3.5 %copy-start.6 = (f32[72,32,128]{0,1,2:T(8,128)S(1)}, f32[72,32,128]{0,1,2:T(8,128)}, u32[]{:S(2)}) copy-start(f32[72,32,128]{0,1,2:T(8,128)} %copy.166) | copy-start | bytes 3538948
  16.0 4.1 %copy-start.8 = (s32[72,32,128]{0,1,2:T(8,128)S(1)}, s32[72,32,128]{0,1,2:T(8,128)}, u32[]{:S(2)}) copy-start(s32[72,32,128]{0,1,2:T(8,128)} %copy.161) | copy-start | bytes 3538948
  16.0 4.7 %copy-start.10 = (f32[72,32,128]{0,1,2:T(8,128)S(1)}, f32[72,32,128]{0,1,2:T(8,128)}, u32[]{:S(2)}) copy-start(f32[72,32,128]{0,1,2:T(8,128)} %copy.162) | copy-start | bytes 3538948
  20.8 1.3 %copy-start.4 = (f32[72,32,128]{0,1,2:T(8,128)}, f32[72,32,128]{0,1,2:T(8,128)S(1)}, u32[]{:S(2)}) copy-start(f32[72,32,128]{0,1,2:T(8,128)S(1)} %get-tuple-element.16) | copy-start | bytes 3538948
  21.6 2.7 %copy-start.2 = (f32[72,32,128]{0,1,2:T(8,128)}, f32[72,32,128]{0,1,2:T(8,128)S(1)}, u32[]{:S(2)}) copy-start(f32[72,32,128]{0,1,2:T(8,128)S(1)} %get-tuple-element.15) | copy-start | bytes 3538948
  21.6 2.7 %copy-start.5 = (f32[72,32,128]{0,1,2:T(8,128)}, f32[72,32,128]{0,1,2:T(8,128)S(1)}, u32[]{:S(2)}) copy-start(f32[72,32,128]{0,1,2:T(8,128)S(1)} %get-tuple-element.14) | copy-start | bytes 3538948
  24.3 23.9 %collective-permute-start.1 = (f32[4,72,2,128]{1,0,2,3:T(4,128)}, f32[4,72,2,128]{1,0,2,3:T(4,128)}, u32[]{:S(2)}, u32[]{:S(2)}) collective-permute-start(f32[4,72,2,128]{1,0,2,3:T(4,128)} %get-tuple-element.25), channel_id=1, source_target_pairs={{2,0},{4,2},{6,4},{8,6},{10,8},{12,10},{14,12},{16,14},{18,16},{20... | collective-permute-start | bytes 884744 | tf_op jit(solution)/shard_map/ppermute | solution.py:19
  25.6 22.6 %collective-permute-start = (f32[4,72,2,128]{1,0,2,3:T(4,128)}, f32[4,72,2,128]{1,0,2,3:T(4,128)}, u32[]{:S(2)}, u32[]{:S(2)}) collective-permute-start(f32[4,72,2,128]{1,0,2,3:T(4,128)} %get-tuple-element.24), channel_id=1, source_target_pairs={{0,2},{2,4},{4,6},{6,8},{8,10},{10,12},{12,14},{14,16},{16,18},{18... | collective-permute-start | bytes 884744 | tf_op jit(solution)/shard_map/ppermute | solution.py:16
  61.4 6.8 %collective-permute-start.2 = (f32[4,72,36,2]{1,0,2,3:T(4,128)S(1)}, f32[4,72,36,2]{1,0,2,3:T(4,128)S(1)}, u32[]{:S(2)}, u32[]{:S(2)}) collective-permute-start(f32[4,72,36,2]{1,0,2,3:T(4,128)S(1)} %get-tuple-element.22), channel_id=1, source_target_pairs={{0,1},{1,0},{2,3},{3,2},{4,5},{5,4},{6,7},{7,6},{8,9},{9,8},{10,11... | collective-permute-start | bytes 248840 | tf_op jit(solution)/shard_map/ppermute | solution.py:16
  63.0 7.5 %collective-permute-start.3 = (f32[4,72,36,2]{1,0,2,3:T(4,128)S(1)}, f32[4,72,36,2]{1,0,2,3:T(4,128)S(1)}, u32[]{:S(2)}, u32[]{:S(2)}) collective-permute-start(f32[4,72,36,2]{1,0,2,3:T(4,128)S(1)} %get-tuple-element.23), channel_id=1, source_target_pairs={{1,0},{0,1},{3,2},{2,3},{5,4},{4,5},{7,6},{6,7},{9,8},{8,9},{11,10... | collective-permute-start | bytes 248840 | tf_op jit(solution)/shard_map/ppermute | solution.py:19
  91.5 4.1 %copy-start.3 = (f32[72,32,128]{0,1,2:T(8,128)S(1)}, f32[72,32,128]{0,1,2:T(8,128)}, u32[]{:S(2)}) copy-start(f32[72,32,128]{0,1,2:T(8,128)} %copy-done.2) | copy-start | bytes 3538948
  91.5 4.1 %copy-start.7 = (f32[72,32,128]{0,1,2:T(8,128)S(1)}, f32[72,32,128]{0,1,2:T(8,128)}, u32[]{:S(2)}) copy-start(f32[72,32,128]{0,1,2:T(8,128)} %copy.166) | copy-start | bytes 3538948
  91.5 4.1 %copy-start.9 = (s32[72,32,128]{0,1,2:T(8,128)S(1)}, s32[72,32,128]{0,1,2:T(8,128)}, u32[]{:S(2)}) copy-start(s32[72,32,128]{0,1,2:T(8,128)} %copy.161) | copy-start | bytes 3538948
  101.3 10.1 %copy-start.1 = (s32[256]{0:T(256)S(1)}, s32[256]{0:T(256)}, u32[]{:S(2)}) copy-start(s32[256]{0:T(256)} %param.17) | copy-start | bytes 3076
where the time goes:
time: 112 us; the launch traced here: 111 us
  other arithmetic  46.4 us (41%)
  local copies, waits for them, and re-layouts  38.5 us (34%)
  blocking collectives  11.5 us (10%)
  starting transfers between devices  7.21 us (6%)
  waiting for transfers between devices  6.93 us (6%)
    unnamed x42, local copies, waits for them, and re-layouts  23.4 us
    concatenate x2, other arithmetic, extended_2(): block = jnp.concatenate([low, block, high], axis=dim)  20.2 us
    all_gather x1, blocking collectives, local(): band = lax.all_gather(fields[:, :, -2:, :], 'lon', axis=3, tiled=True)  11.5 us
    slice x1, local copies, waits for them, and re-layouts, local(): extended[1]  7.15 us
    mul x1, other arithmetic, local(): northward_transport_rate * (vm + time_step * trend_v / volv)  7.01 us
    ppermute x2, starting transfers between devices, extended_2(): lax.ppermute(lax.slice_in_dim(block, block.shape[dim] - width, None, axis...  5.39 us
    ppermute x2, waiting for transfers between devices, extended_2(): lax.ppermute(lax.slice_in_dim(block, block.shape[dim] - width, None, axis...  4.69 us
    mul x1, other arithmetic, advect(): 0.5 * (cx(tuv, 2, 1) + cx(tuv, 3, 1))  4.68 us
  transfers between devices with their start and end apart: 4, of which 2 were waited for; matrix products, arithmetic and copies ran while one was open for 6% of the time, Pallas kernels for 0%

commit v1 on v0

v1 whole, which is shorter than its diff:
```python
import functools

import jax
import jax.numpy as jnp
from jax import lax
from jax.experimental import pallas as pl
from jax.experimental.pallas import tpu as pltpu
from jax.sharding import PartitionSpec as P

time_step = 0.2
lanes = 128
group = 8
spare = 8
MESH = pl.DeviceIdType.MESH


def chunk_count(levels):
    groups = levels // group
    return next(c for c in (3, 2, 1) if groups % c == 0)


def roll(x, shift):
    return pltpu.roll(x, shift % lanes, 1)


def exchange_kernel(
    nlat, nlon, levels, rows,
    u_hbm, v_hbm, eu_hbm, ev_hbm, su_hbm, sv_hbm, mu_hbm, mv_hbm,
    um_x, vm_x, tu_x, tv_x, cu_x, cv_x, packs, corner_u, corner_v, band,
    u_in, v_in, eu_in, ev_in, su_in, sv_in, mu_in, mv_in,
    pack_own, corner_u_own, corner_v_own,
    load_sem, span_sem, up_send, up_recv, down_send, down_recv,
    lon_send, lon_recv, diag_send, diag_recv, band_send, band_recv,
):
    chunks = chunk_count(levels)
    depth = levels // chunks
    lat = lax.axis_index("lat")
    lon = lax.axis_index("lon")
    right = lax.rem(lon + 1, nlon)
    left = lax.rem(lon + nlon - 1, nlon)
    has_up = lat < nlat - 1
    has_down = lat > 0
    sides = 1 if nlon == 2 else 2

    pairs = (
        (u_hbm, u_in), (mu_hbm, mu_in), (eu_hbm, eu_in),
        (v_hbm, v_in), (mv_hbm, mv_in), (ev_hbm, ev_in),
    )
    spans = [
        pltpu.make_async_copy(su_hbm, su_in, span_sem.at[0]),
        pltpu.make_async_copy(sv_hbm, sv_in, span_sem.at[1]),
    ]
    loads = [
        [
            pltpu.make_async_copy(
                a.at[pl.ds(c * depth, depth)], b.at[pl.ds(c * depth, depth), pl.ds(0, rows)], load_sem.at[c, k]
            )
            for k, (a, b) in enumerate(pairs)
        ]
        for c in range(chunks)
    ]
    for copy in spans:
        copy.start()
    for per_chunk in loads:
        for copy in per_chunk:
            copy.start()

    barrier = pltpu.get_barrier_semaphore()

    def greet(where):
        pl.semaphore_signal(barrier, inc=1, device_id=where, device_id_type=MESH)

    greet((lat, right))
    if nlon > 2:
        greet((lat, left))

    @pl.when(has_up)
    def _():
        greet((lat + 1, lon))
        greet((lat + 1, left))

    @pl.when(has_down)
    def _():
        greet((lat - 1, lon))
        greet((lat - 1, right))

    if nlon > 3:
        @pl.when(lat == nlat - 1)
        def _():
            for d in range(2, nlon - 1):
                greet((lat, lax.rem(lon + d, nlon)))

    def arrive():
        @pl.when(lat == 0)
        def _():
            pl.semaphore_wait(barrier, sides + 2)

        @pl.when(has_up & has_down)
        def _():
            pl.semaphore_wait(barrier, sides + 4)

        @pl.when(lat == nlat - 1)
        def _():
            pl.semaphore_wait(barrier, sides + 2 + max(nlon - 3, 0))

    def remote(src, dst, send, recv, where):
        return pltpu.make_async_remote_copy(
            src_ref=src, dst_ref=dst, send_sem=send, recv_sem=recv,
            device_id=where, device_id_type=MESH,
        )

    def up_copies(c):
        part = pl.ds(c * depth, depth)
        where = (lat + 1, lon)
        moves = (
            (um_x.at[pl.ds(rows, 2), part], um_x.at[pl.ds(0, 2), part]),
            (vm_x.at[pl.ds(rows, 2), part], vm_x.at[pl.ds(0, 2), part]),
            (tv_x.at[pl.ds(rows, 1), part], tv_x.at[pl.ds(0, 1), part]),
        )
        return [
            remote(a, b, up_send.at[c, k], up_recv.at[c, k], where)
            for k, (a, b) in enumerate(moves)
        ]

    def down_copies(c):
        part = pl.ds(c * depth, depth)
        where = (lat - 1, lon)
        moves = (
            (um_x.at[pl.ds(2, 2), part], um_x.at[pl.ds(rows + 2, 2), part]),
            (vm_x.at[pl.ds(2, 2), part], vm_x.at[pl.ds(rows + 2, 2), part]),
            (tu_x.at[pl.ds(0, 1), part], tu_x.at[pl.ds(rows, 1), part]),
            (tv_x.at[pl.ds(1, 1), part], tv_x.at[pl.ds(rows + 1, 1), part]),
        )
        return [
            remote(a, b, down_send.at[c, k], down_recv.at[c, k], where)
            for k, (a, b) in enumerate(moves)
        ]

    def lon_copies(c):
        part = pl.ds(c * depth, depth)
        targets = (right,) if nlon == 2 else (right, left)
        return [
            remote(
                pack_own.at[:, part], packs.at[k, :, part],
                lon_send.at[c, k], lon_recv.at[c, k], (lat, target),
            )
            for k, target in enumerate(targets)
        ]

    def corner_down():
        return remote(
            corner_u_own, corner_u, diag_send.at[0], diag_recv.at[0], (lat - 1, right)
        )

    def corner_up():
        return remote(
            corner_v_own, corner_v, diag_send.at[1], diag_recv.at[1], (lat + 1, left)
        )

    def band_copy(c, d):
        part = pl.ds(c * depth, depth)
        return remote(
            band.at[lon, :, part], band.at[lon, :, part],
            band_send.at[c, d], band_recv.at[c, d], (lat, lax.rem(lon + d, nlon)),
        )

    def band_arrival(c, d):
        part = pl.ds(c * depth, depth)
        origin = lax.rem(lon + nlon - d, nlon)
        return remote(
            band.at[lon, :, part], band.at[origin, :, part],
            band_send.at[c, d], band_recv.at[c, d], (lat, lax.rem(lon + d, nlon)),
        )

    lane = lax.broadcasted_iota(jnp.int32, (group, lanes), 1)
    quad = lane // 4
    place = lane % 4
    pitch = rows + spare
    views = [ref.reshape(levels * pitch, lanes) for _, ref in pairs]

    def compute(g, corners):
        cu_corner, cv_corner = corners
        base = g * group
        part = pl.ds(pl.multiple_of(base, group), group)
        zero = jnp.zeros((group, lanes), jnp.float32)
        pack_u, pack_v, pack_t = zero, zero, zero
        for r in range(rows):
            u, mu, eu, v, mv, ev = [
                view[pl.ds(base * pitch + r, group, stride=pitch), :] for view in views
            ]
            mu = mu.astype(jnp.float32)
            mv = mv.astype(jnp.float32)
            um = mu * u
            vm = mv * v
            vol_u = su_in[pl.ds(r, 1), :] * eu
            vol_v = sv_in[pl.ds(r, 1), :] * ev
            tu = vol_u * um
            tv = vol_v * vm
            um_x[r + 2, part, :] = um
            vm_x[r + 2, part, :] = vm
            tu_x[r, part, :] = tu
            tv_x[r + 1, part, :] = tv
            cu_x[r, part, :] = mu * (-time_step / 24.0) / vol_u
            cv_x[r, part, :] = mv * (-time_step / 24.0) / vol_v
            here = quad == r
            pack_u = jnp.where(here, roll(um, 2 + 4 * r), pack_u)
            pack_v = jnp.where(here, roll(vm, 2 + 4 * r), pack_v)
            both = jnp.where(place < 2, roll(tu, 1 + 4 * r), roll(tv, 3 + 4 * r))
            pack_t = jnp.where(here, both, pack_t)
            if r == 0:
                cu_corner = jnp.where(lane == g, pltpu.roll(tu, g + 1, 1), cu_corner)
            if r == rows - 1:
                cv_corner = jnp.where(lane == g, pltpu.roll(tv, g, 1), cv_corner)
                band[lon, 4, part, :] = tu
                band[lon, 5, part, :] = tv
            if r >= rows - 2:
                band[lon, r - rows + 2, part, :] = um
                band[lon, r - rows + 4, part, :] = vm
        pack_own[0, part, :] = pack_u
        pack_own[1, part, :] = pack_v
        pack_own[2, part, :] = pack_t
        return cu_corner, cv_corner

    @pl.when(lat == 0)
    def _():
        um_x[pl.ds(0, 2)] = jnp.zeros((2, levels, lanes), jnp.float32)
        vm_x[pl.ds(0, 2)] = jnp.zeros((2, levels, lanes), jnp.float32)
        tv_x[pl.ds(0, 1)] = jnp.zeros((1, levels, lanes), jnp.float32)
        corner_v[...] = jnp.zeros((group, lanes), jnp.float32)

    for copy in spans:
        copy.wait()
    corners = (jnp.zeros((group, lanes), jnp.float32),) * 2
    for c in range(chunks):
        for copy in loads[c]:
            copy.wait()
        per = depth // group
        corners = lax.fori_loop(c * per, (c + 1) * per, compute, corners)
        if c == 0:
            arrive()

        for copy in lon_copies(c):
            copy.start()

        @pl.when(has_down)
        def _():
            for copy in down_copies(c):
                copy.start()

        @pl.when(has_up)
        def _():
            for copy in up_copies(c):
                copy.start()

        @pl.when(lat == nlat - 1)
        def _():
            for d in range(1, nlon):
                band_copy(c, d).start()

    corner_u_own[...], corner_v_own[...] = corners

    @pl.when(has_down)
    def _():
        corner_down().start()

    @pl.when(has_up)
    def _():
        corner_up().start()

    for c in range(chunks):
        for copy in lon_copies(c):
            copy.wait()

        @pl.when(has_down)
        def _():
            for copy in down_copies(c):
                copy.wait_send()
            for copy in up_copies(c):
                copy.wait_recv()

        @pl.when(has_up)
        def _():
            for copy in up_copies(c):
                copy.wait_send()
            for copy in down_copies(c):
                copy.wait_recv()

        @pl.when(lat == nlat - 1)
        def _():
            for d in range(1, nlon):
                band_copy(c, d).wait_send()
                band_arrival(c, d).wait_recv()

    @pl.when(has_down)
    def _():
        corner_down().wait_send()
        corner_up().wait_recv()

    @pl.when(has_up)
    def _():
        corner_up().wait_send()
        corner_down().wait_recv()


def stencil_kernel(
    nlat, nlon, levels, rows,
    fold_ref, um_x, vm_x, tu_x, tv_x, cu_x, cv_x, packs, corner_u, corner_v, band,
    u_out, v_out,
    high, high_left, beside, moved, u_buf, v_buf, out_sem,
):
    lat = lax.axis_index("lat")
    lon = lax.axis_index("lon")
    groups = levels // group
    width = nlon * lanes
    lane = lax.broadcasted_iota(jnp.int32, (group, lanes), 1)
    top = lat == nlat - 1

    @pl.when(top)
    def _():
        first = fold_ref[0]
        own = lax.rem(first - lon * lanes - lane + 2 * width, width)
        before = jnp.zeros_like(lane) + lax.rem(first - lon * lanes + 1 + 2 * width, width)

        def pick(k, part, index):
            block = index // lanes
            spot = index % lanes
            got = jnp.zeros((group, lanes), jnp.float32)
            for b in range(nlon):
                taken = jnp.take_along_axis(
                    band[b, k, part, :], spot, axis=1, mode="promise_in_bounds"
                )
                got = jnp.where(block == b, taken, got)
            return -got

        def fill(g, carry):
            part = pl.ds(pl.multiple_of(g * group, group), group)
            high[0, part, :] = pick(1, part, own)
            high[1, part, :] = pick(0, part, own)
            high[2, part, :] = pick(3, part, own)
            high[3, part, :] = pick(2, part, own)
            high[4, part, :] = pick(4, part, own)
            high[5, part, :] = pick(5, part, own)
            high_left[part, :] = pick(4, part, before)
            return carry

        lax.fori_loop(0, groups, fill, 0)

    @pl.when(lat < nlat - 1)
    def _():
        def fill(g, carry):
            part = pl.ds(pl.multiple_of(g * group, group), group)
            high[0, part, :] = um_x[rows + 2, part, :]
            high[1, part, :] = um_x[rows + 3, part, :]
            high[2, part, :] = vm_x[rows + 2, part, :]
            high[3, part, :] = vm_x[rows + 3, part, :]
            high[4, part, :] = tu_x[rows, part, :]
            high[5, part, :] = tv_x[rows + 1, part, :]
            high_left[part, :] = pltpu.roll(corner_u[...], lanes - 1 - g, 1)
            return carry

        lax.fori_loop(0, groups, fill, 0)

    place = lane % 4
    pitch = rows + spare
    u_view = u_buf.reshape(levels * pitch, lanes)
    v_view = v_buf.reshape(levels * pitch, lanes)

    def q(a, b, c, d):
        return 7.0 * (b + c) - (a + d)

    def out_copies(g):
        part = pl.ds(g * group, group)
        return (
            pltpu.make_async_copy(u_buf.at[part, pl.ds(0, rows)], u_out.at[part], out_sem.at[g, 0]),
            pltpu.make_async_copy(v_buf.at[part, pl.ds(0, rows)], v_out.at[part], out_sem.at[g, 1]),
        )

    def readers(part):
        def um(j):
            return um_x[j + 2, part, :] if j < rows else high[j - rows, part, :]

        def vm(j):
            return vm_x[j + 2, part, :] if j < rows else high[j - rows + 2, part, :]

        def tu(j):
            return tu_x[j, part, :] if j < rows else high[4, part, :]

        def tv(j):
            return tv_x[j + 1, part, :] if j < rows else high[5, part, :]

        return um, vm, tu, tv

    def unpack(g, carry):
        part = pl.ds(pl.multiple_of(g * group, group), group)
        if packs.shape[0] == 1:
            pack_u, pack_v, pack_t = [packs[0, k, part, :] for k in range(3)]
        else:
            pack_u, pack_v = [
                jnp.where(place < 2, packs[0, k, part, :], packs[1, k, part, :])
                for k in range(2)
            ]
            pack_t = jnp.where(place < 1, packs[0, 2, part, :], packs[1, 2, part, :])
        for j in range(rows):
            beside[0, j, part, :] = roll(pack_u, -(4 * j + 2))
            beside[1, j, part, :] = roll(pack_v, -(4 * j + 2))
            beside[2, j, part, :] = roll(pack_t, -(4 * j + 1))
            beside[3, j, part, :] = roll(pack_t, -(4 * j + 3))
        return carry

    lax.fori_loop(0, groups, unpack, 0)

    def shift(g, carry):
        part = pl.ds(pl.multiple_of(g * group, group), group)
        um, vm, tu, tv = readers(part)
        tv_low = jnp.where(
            lane == 0, pltpu.roll(corner_v[...], lax.rem(lanes - g, lanes), 1), tv(-1)
        )
        moved[11, 0, part, :] = roll(tv_low, -1)
        moved[11, 1, part, :] = roll(
            jnp.where(lane == lanes - 1, high_left[part, :], tu(rows)), 1
        )
        for j in range(rows):
            for k, own in ((0, um(j)), (4, vm(j))):
                halo = beside[k // 4, j, part, :]
                low = jnp.where(lane >= lanes - 2, halo, own)
                upper = jnp.where(lane < 2, halo, own)
                moved[k, j, part, :] = roll(low, 2)
                moved[k + 1, j, part, :] = roll(jnp.where(lane == lanes - 1, halo, own), 1)
                moved[k + 2, j, part, :] = roll(jnp.where(lane == 0, halo, own), -1)
                moved[k + 3, j, part, :] = roll(upper, -2)
            own, halo = tu(j), beside[2, j, part, :]
            moved[8, j, part, :] = roll(jnp.where(lane == lanes - 1, halo, own), 1)
            moved[9, j, part, :] = roll(jnp.where(lane == 0, halo, own), -1)
            moved[10, j, part, :] = roll(jnp.where(lane == 0, beside[3, j, part, :], tv(j)), -1)
        return carry

    lax.fori_loop(0, groups, shift, 0)

    def step(g, carry):
        part = pl.ds(pl.multiple_of(g * group, group), group)
        um, vm, tu, tv = readers(part)

        def tu_sides(j):
            if j < rows:
                return tu(j), moved[8, j, part, :], moved[9, j, part, :]
            return tu(j), moved[11, 1, part, :], None

        def around(k, j, own):
            w2, w1, e1, e2 = [moved[k + i, j, part, :] for i in range(4)]
            return q(w2, w1, own, e1), q(w1, own, e1, e2)

        def fvf(j):
            east = moved[11, 0, part, :] if j < 0 else moved[10, j, part, :]
            return (tv(j) + east) * q(um(j - 1), um(j), um(j + 1), um(j + 2))

        def fvt(j):
            return (tv(j - 1) + tv(j)) * q(vm(j - 2), vm(j - 1), vm(j), vm(j + 1))

        fvf_low = fvf(-1)
        fvt_low = fvt(0)
        tu_own, tu_west, tu_east = tu_sides(0)
        for j in range(rows):
            fvf_high = fvf(j)
            fvt_high = fvt(j + 1)
            um_own = um(j)
            vm_own = vm(j)
            q_west, q_east = around(0, j, um_own)
            du = (tu_own + tu_east) * q_east - (tu_west + tu_own) * q_west
            du = du + (fvf_high - fvf_low)
            next_own, next_west, next_east = tu_sides(j + 1)
            q_west, q_east = around(4, j, vm_own)
            dv = (tu_own + next_own) * q_east - (tu_west + next_west) * q_west
            dv = dv + (fvt_high - fvt_low)
            where = pl.ds(g * (group * pitch) + j, group, stride=pitch)
            u_view[where, :] = um_own + cu_x[j, part, :] * du
            v_view[where, :] = vm_own + cv_x[j, part, :] * dv
            fvf_low, fvt_low = fvf_high, fvt_high
            tu_own, tu_west, tu_east = next_own, next_west, next_east
        for copy in out_copies(g):
            copy.start()
        return carry

    lax.fori_loop(0, groups, step, 0)

    def finish(g, carry):
        for copy in out_copies(g):
            copy.wait()
        return carry

    lax.fori_loop(0, groups, finish, 0)


def local(nlat, nlon, u, v, eu, ev, su, sv, mu, mv, fold):
    u, v, eu, ev, su, sv, mu, mv = [
        pltpu.with_memory_space_constraint(x, pltpu.HBM) for x in (u, v, eu, ev, su, sv, mu, mv)
    ]
    levels, rows, _ = u.shape
    chunks = chunk_count(levels)
    sides = 1 if nlon == 2 else 2
    f32 = jnp.float32
    vmem = pl.BlockSpec(memory_space=pltpu.VMEM)
    hbm = pl.BlockSpec(memory_space=pltpu.HBM)
    shapes = [
        (rows + 4, levels, lanes),
        (rows + 4, levels, lanes),
        (rows + 1, levels, lanes),
        (rows + 2, levels, lanes),
        (rows, levels, lanes),
        (rows, levels, lanes),
        (sides, 3, levels, lanes),
        (group, lanes),
        (group, lanes),
        (nlon, 6, levels, lanes),
    ]
    block = (levels, rows, lanes)
    roomy = (levels, rows + spare, lanes)
    dma = pltpu.SemaphoreType.DMA
    fields = pl.pallas_call(
        functools.partial(exchange_kernel, nlat, nlon, levels, rows),
        out_shape=[pltpu.VMEM(s, f32) for s in shapes],
        in_specs=[hbm] * 8,
        out_specs=[vmem] * len(shapes),
        scratch_shapes=[
            pltpu.VMEM(roomy, f32),
            pltpu.VMEM(roomy, f32),
            pltpu.VMEM(roomy, f32),
            pltpu.VMEM(roomy, f32),
            pltpu.VMEM((rows, lanes), f32),
            pltpu.VMEM((rows, lanes), f32),
            pltpu.VMEM(roomy, jnp.int32),
            pltpu.VMEM(roomy, jnp.int32),
            pltpu.VMEM((3, levels, lanes), f32),
            pltpu.VMEM((group, lanes), f32),
            pltpu.VMEM((group, lanes), f32),
            dma((chunks, 6)),
            dma((2,)),
            dma((chunks, 3)),
            dma((chunks, 3)),
            dma((chunks, 4)),
            dma((chunks, 4)),
            dma((chunks, sides)),
            dma((chunks, sides)),
            dma((2,)),
            dma((2,)),
            dma((chunks, nlon)),
            dma((chunks, nlon)),
        ],
        compiler_params=pltpu.CompilerParams(
            collective_id=0, has_side_effects=True, vmem_limit_bytes=16 * 1024 * 1024
        ),
        name="exchange",
    )(u, v, eu, ev, su, sv, mu, mv)
    result = pl.pallas_call(
        functools.partial(stencil_kernel, nlat, nlon, levels, rows),
        out_shape=[jax.ShapeDtypeStruct(block, f32)] * 2,
        in_specs=[pl.BlockSpec(memory_space=pltpu.SMEM)] + [vmem] * len(shapes),
        out_specs=[hbm] * 2,
        scratch_shapes=[
            pltpu.VMEM((6, levels, lanes), f32),
            pltpu.VMEM((levels, lanes), f32),
            pltpu.VMEM((4, rows, levels, lanes), f32),
            pltpu.VMEM((12, rows, levels, lanes), f32),
            pltpu.VMEM(roomy, f32),
            pltpu.VMEM(roomy, f32),
            dma((levels // group, 2)),
        ],
        compiler_params=pltpu.CompilerParams(vmem_limit_bytes=32 * 1024 * 1024),
        name="stencil",
    )(fold, *fields)
    return tuple(result)


def solution(mesh):
    level_rows_columns = P(None, "lat", "lon")
    return jax.shard_map(
        functools.partial(local, mesh.shape["lat"], mesh.shape["lon"]),
        mesh=mesh,
        in_specs=(
            level_rows_columns,
            level_rows_columns,
            level_rows_columns,
            level_rows_columns,
            P("lat", "lon"),
            P("lat", "lon"),
            level_rows_columns,
            level_rows_columns,
            P(),
        ),
        out_specs=(level_rows_columns,) * 2,
        check_vma=False,
    )
```

time: 112 us -> 22.4 us (0.20)
  the two profiles are of different devices: /device:TPU:0 before, /device:TPU:29 now
where the time goes in v1:
time: 22.4 us; the launch traced here: 22.2 us
  Pallas kernels  21.6 us (96%)
  between operations  0.66 us (3%)
    pallas_call x1, Pallas kernels, local(): pl.pallas_call(functools.partial(exchange_kernel, nlat, nlon, levels, row...  11.2 us
    pallas_call x1, Pallas kernels, local(): pl.pallas_call(functools.partial(stencil_kernel, nlat, nlon, levels, rows...  10.3 us

profile of v1, /device:TPU:29, one launch (start us, length us, event | category | flops | bytes accessed | tf_op | source)
XLA Modules:
  0.0 22.2 jit_solution(5318723377971563219)
XLA Ops:
  0.6 0.0 copy-start
  0.6 11.2 %exchange.1 = (f32[36,72,128]{2,1,0:T(8,128)S(1)}, f32[36,72,128]{2,1,0:T(8,128)S(1)}, f32[33,72,128]{2,1,0:T(8,128)S(1)}, f32[34,72,128]{2,1,0:T(8,128)S(1)}, f...) custom-call(f32[72,32,128]{2,1,0:T(8,128)} %u_hbm.1, ...), custom_call_target="tpu_custom_call" | custom-call | tf_op jit(solution)/shard_map/exchange/pallas_call | solution.py:518
  11.9 0.0 copy-done
  11.9 10.3 %stencil.1 = (f32[72,32,128]{2,1,0:T(8,128)}, f32[72,32,128]{2,1,0:T(8,128)}) custom-call(s32[256]{0:T(256)S(1)} %copy-done, f32[36,72,128]{2,1,0:T(8,128)S(1)} %get-tuple-element.12.um_x, f32[36,72,128]{2,1,0:T(8,128)S(1)} %get-tuple-element.13.vm_x, f32[33,72,128]{2,1,0:T(8,128)S(1)} %get-tuple-element.14.tu_x, f32[34,72,128]{2,1,0:T(8,128)S(1)} %get-tuple-element.15.tv_x, ...), custom_call_target="tpu_custom_call" | custom-call | tf_op jit(solution)/shard_map/stencil/pallas_call | solution.py:553
Async XLA Ops:
  0.6 11.3 %copy-start = (s32[256]{0:T(256)S(1)}, s32[256]{0:T(256)}, u32[]{:S(2)}) copy-start(s32[256]{0:T(256)} %fold_ref.1) | copy-start | bytes 3076
